TPU v7x, 32 devices: a whole 2x2x4 slice. The times are simulated.
32 devices in a mesh: ka: 8 (over y, x, core), ga: 4 (over z).
Axes of the slice: x: 2, y: 2, z: 4, core: 2. Of those that a mesh axis runs over, the one named last changes fastest.
Arguments:
- pair_densities: float32 [8192, 8192], P('ka', 'ga'), may hold values from -0.0625 to 0.0625
- energies: float32 [8192], P('ka'), may hold values from -2 to 2
- coulomb: float32 [8192], P('ga'), may hold values from 0.2 to 2
- start: float32 [8192, 128], P('ka'), may hold values from -6 to 6
Outputs:
- alphas: float32 [4, 128], replicated
- betas: float32 [4, 128], replicated
- lanczos_vector: float32 [8192, 128], P('ka')
All inputs are finite; a program needn't handle non-finite values.
Results may differ from a plain program's by a relative error of at most 0.00013.
Values sent between devices are 32-bit elements; how exact they have to be, the bound alone decides.
A program may use at most 64 MiB of HBM per device.

v0:
```python
import jax
import jax.numpy as jnp
from jax import lax
from jax.sharding import PartitionSpec as P

ITERS = 4


EPSILON = 1e-06


def per_device(pair_densities, energies, coulomb, start):
    precise = lax.Precision.HIGHEST
    vector_count = start.shape[1]

    def project(full_vector, extra_rows):
        projected = jnp.dot(
            pair_densities.T, full_vector, precision=precise, preferred_element_type=jnp.float32
        )
        projected = jnp.concatenate([projected] + extra_rows, axis=0)
        return lax.psum(projected, "ka")

    start_sq = lax.psum(jnp.sum(start * start, axis=0), "ka")
    full_vector = start / jnp.sqrt(start_sq + EPSILON)
    vector = full_vector
    previous = jnp.zeros_like(vector)
    beta_now = jnp.zeros((vector_count,), jnp.float32)
    alpha_rows = []
    beta_rows = []
    remainder_full = full_vector
    remainder_own = vector
    for step in range(ITERS):
        energy_row = jnp.sum(energies[:, None] * remainder_full * remainder_full, axis=0)[None, :]
        if step == 0:
            summed = project(remainder_full, [energy_row])
            projected = summed[:-1]
            energy_sum = summed[-1]
            vector = remainder_own
        else:
            square_row = jnp.sum(remainder_full * remainder_full, axis=0)[None, :]
            summed = project(remainder_full, [square_row, energy_row])
            beta_full = jnp.sqrt(summed[-2] + EPSILON)
            projected = summed[:-2] / beta_full
            energy_sum = summed[-1] / (beta_full * beta_full)
            beta_new = beta_full
            beta_rows.append(beta_new)
            previous = vector
            vector = remainder_own / beta_new
            beta_now = beta_new
        weighted = coulomb[:, None] * projected
        curvature = jnp.sum(projected * weighted, axis=0)[None, :]
        partial_value = jnp.dot(
            pair_densities, weighted, precision=precise, preferred_element_type=jnp.float32
        )
        combine_partial_value = jnp.concatenate([partial_value, curvature], axis=0)
        combined = lax.psum(combine_partial_value, "ga")
        mixed = combined[:-1]
        alpha_now = energy_sum + combined[-1]
        image = energies[:, None] * vector + mixed
        remainder_own = image - alpha_now * vector - beta_now * previous
        alpha_rows.append(alpha_now)
        if step + 1 < ITERS:
            remainder_full = remainder_own
    last_sq = lax.psum(jnp.sum(remainder_own * remainder_own, axis=0), "ka")
    beta_new = jnp.sqrt(last_sq + EPSILON)
    beta_rows.append(beta_new)
    vector = remainder_own / beta_new
    alpha_table = jnp.stack(alpha_rows)
    beta_table = jnp.stack(beta_rows)
    full_vector = vector
    return (alpha_table, beta_table, full_vector)


def solution(mesh):
    placed = (P("ka", "ga"), P("ka"), P("ga"), P("ka", None))
    return jax.shard_map(
        per_device, mesh=mesh, in_specs=placed, out_specs=(P(), P(), P("ka", None)), check_vma=False
    )
```

profile of v0, /device:TPU:0, one launch (start us, length us, event | category | flops | bytes accessed | tf_op | source)
XLA Modules:
  0.0 530.7 jit_solution(17635808133581083179)
XLA Ops:
  9.7 15.2 %psum.70 = f32[128]{0:T(128)S(1)} all-reduce(f32[128]{0:T(128)S(1)} %multiply_reduce_fusion.4), channel_id=1, replica_groups=mesh['ka'=8,'ga'=4] {'ka'}, use_global_device_ids=true, to_apply=%region_1.0 | all-reduce | flops 128 | bytes 1024 | tf_op jit(solution)/shard_map/psum | solution.py:23
  25.2 7.1 %convolution_bitcast_fusion.3 = f32[2048,128]{0,1:T(8,128)S(1)} fusion(f32[1024,2048]{1,0:T(8,128)} %param.4, f32[1024,128]{0,1:T(8,128)S(1)} %copy.39, f32[128]{0:T(128)S(1)} %add_sqrt_fusion.1), kind=kOutput, calls=%fused_computation.3 | convolution fusion | flops 3221356544 | bytes 9961984 | tf_op jit(solution)/shard_map/dot_general | solution.py:17
  33.4 56.5 %all-reduce.9.cloned.1.call-done = f32[2049,128]{0,1:T(8,128)} async-done(((f32[2049,128]{0,1:T(8,128)}), f32[2049,128]{0,1:T(8,128)}) %all-reduce.9.cloned.1.call-update) | async-done | bytes 1049104 | tf_op jit(solution)/shard_map/psum | solution.py:21
  89.9 1.5 fusion.20
  91.5 11.1 %fusion.8 = f32[1024,128]{0,1:T(8,128)S(1)} fusion(f32[1024,2048]{1,0:T(8,128)} %param.4, f32[2049,128]{0,1:T(8,128)S(1)} %copy-done.3, f32[2048]{0:T(1024)S(1)} %copy-done.4), kind=kOutput, calls=%fused_computation.16 | convolution fusion | flops 3221487616 | bytes 9969664 | tf_op jit(solution)/shard_map/dot_general | solution.py:52
  103.6 39.1 %all-reduce.11.cloned.1.call-done = f32[1025,128]{0,1:T(8,128)} async-done(((f32[1025,128]{0,1:T(8,128)}), f32[1025,128]{0,1:T(8,128)}) %all-reduce.11.cloned.1.call-update) | async-done | bytes 524816 | tf_op jit(solution)/shard_map/psum | solution.py:56
  145.2 7.0 %convolution_bitcast_fusion.2 = f32[2048,128]{0,1:T(8,128)S(1)} fusion(f32[1024,128]{0,1:T(8,128)S(1)} %get-tuple-element.28, f32[1024,2048]{1,0:T(8,128)} %param.4), kind=kOutput, calls=%fused_computation.2 | convolution fusion | flops 3221225472 | bytes 9961472 | tf_op jit(solution)/shard_map/dot_general | solution.py:17
  153.7 56.4 %all-reduce.13.cloned.1.call-done = f32[2050,128]{0,1:T(8,128)} async-done(((f32[2050,128]{0,1:T(8,128)}), f32[2050,128]{0,1:T(8,128)}) %all-reduce.13.cloned.1.call-update) | async-done | bytes 1049616 | tf_op jit(solution)/shard_map/psum | solution.py:21
  211.2 1.5 fusion.21
  212.8 10.9 %fusion.11 = f32[1024,128]{0,1:T(8,128)S(1)} fusion(f32[1024,2048]{1,0:T(8,128)} %param.4, f32[2048]{0:T(1024)S(1)} %copy-done.4, f32[2050,128]{0,1:T(8,128)S(1)} %copy-done.1, f32[128]{0:T(128)S(1)} %get-tuple-element.32), kind=kOutput, calls=%fused_computation.17 | convolution fusion | flops 3221749760 | bytes 9970176 | tf_op jit(solution)/shard_map/dot_general | solution.py:52
  224.6 39.0 %all-reduce.15.cloned.1.call-done = f32[1025,128]{0,1:T(8,128)} async-done(((f32[1025,128]{0,1:T(8,128)}), f32[1025,128]{0,1:T(8,128)}) %all-reduce.15.cloned.1.call-update) | async-done | bytes 524816 | tf_op jit(solution)/shard_map/psum | solution.py:56
  264.7 1.4 fusion.28
  266.4 7.0 %convolution_bitcast_fusion.1 = f32[2048,128]{0,1:T(8,128)S(1)} fusion(f32[1024,128]{0,1:T(8,128)S(1)} %get-tuple-element.25, f32[1024,2048]{1,0:T(8,128)} %param.4), kind=kOutput, calls=%fused_computation.1 | convolution fusion | flops 3221225472 | bytes 9961472 | tf_op jit(solution)/shard_map/dot_general | solution.py:17
  274.7 56.6 %all-reduce.17.cloned.1.call-done = f32[2050,128]{0,1:T(8,128)} async-done(((f32[2050,128]{0,1:T(8,128)}), f32[2050,128]{0,1:T(8,128)}) %all-reduce.17.cloned.1.call-update) | async-done | bytes 1049616 | tf_op jit(solution)/shard_map/psum | solution.py:21
  332.4 1.5 fusion.22
  334.0 10.9 %fusion.14 = f32[1024,128]{0,1:T(8,128)S(1)} fusion(f32[1024,2048]{1,0:T(8,128)} %param.4, f32[2048]{0:T(1024)S(1)} %copy-done.4, f32[2050,128]{0,1:T(8,128)S(1)} %copy-done.2, f32[128]{0:T(128)S(1)} %get-tuple-element.34), kind=kOutput, calls=%fused_computation.18 | convolution fusion | flops 3221749760 | bytes 9970176 | tf_op jit(solution)/shard_map/dot_general | solution.py:52
  346.1 38.8 %all-reduce.19.cloned.1.call-done = f32[1025,128]{0,1:T(8,128)} async-done(((f32[1025,128]{0,1:T(8,128)}), f32[1025,128]{0,1:T(8,128)}) %all-reduce.19.cloned.1.call-update) | async-done | bytes 524816 | tf_op jit(solution)/shard_map/psum | solution.py:56
  385.9 1.4 fusion.29
  387.6 7.0 %convolution_bitcast_fusion = f32[2048,128]{0,1:T(8,128)S(1)} fusion(f32[1024,128]{0,1:T(8,128)S(1)} %get-tuple-element.22, f32[1024,2048]{1,0:T(8,128)} %param.4), kind=kOutput, calls=%fused_computation | convolution fusion | flops 3221225472 | bytes 9961472 | tf_op jit(solution)/shard_map/dot_general | solution.py:17
  395.9 56.6 %all-reduce.21.cloned.1.call-done = f32[2050,128]{0,1:T(8,128)} async-done(((f32[2050,128]{0,1:T(8,128)}), f32[2050,128]{0,1:T(8,128)}) %all-reduce.21.cloned.1.call-update) | async-done | bytes 1049616 | tf_op jit(solution)/shard_map/psum | solution.py:21
  453.6 1.5 fusion.23
  455.2 10.9 %fusion.17 = f32[1024,128]{0,1:T(8,128)S(1)} fusion(f32[1024,2048]{1,0:T(8,128)} %param.4, f32[2048]{0:T(1024)S(1)} %copy-done.4, f32[2050,128]{0,1:T(8,128)S(1)} %copy-done, f32[128]{0:T(128)S(1)} %get-tuple-element.36), kind=kOutput, calls=%fused_computation.19 | convolution fusion | flops 3221749760 | bytes 9970176 | tf_op jit(solution)/shard_map/dot_general | solution.py:52
  467.5 38.6 %all-reduce.23.cloned.1.call-done = f32[1025,128]{0,1:T(8,128)} async-done(((f32[1025,128]{0,1:T(8,128)}), f32[1025,128]{0,1:T(8,128)}) %all-reduce.23.cloned.1.call-update) | async-done | bytes 524816 | tf_op jit(solution)/shard_map/psum | solution.py:56
  508.5 13.0 %psum.79 = f32[128]{0:T(128)S(1)} all-reduce(f32[128]{0:T(128)S(1)} %get-tuple-element.18), channel_id=1, replica_groups=mesh['ka'=8,'ga'=4] {'ka'}, use_global_device_ids=true, to_apply=%region_22.0 | all-reduce | flops 128 | bytes 1024 | tf_op jit(solution)/shard_map/psum | solution.py:64
  (72 shorter events, 25.7 us)
Async XLA Ops:
  7.2 17.7 %copy-start.5 = (f32[1024]{0:T(1024)S(1)}, f32[1024]{0:T(1024)}, u32[]{:S(2)}) copy-start(f32[1024]{0:T(1024)} %param.5) | copy-start | bytes 12292
  7.2 82.7 %all-reduce.9.cloned.1.call-start = ((), (), s32[]{:S(2)}) async-start(), calls=%async_computation | async-start | bytes 2228224 | tf_op jit(solution)/shard_map/psum | solution.py:21
  33.4 56.6 %copy-start.4 = (f32[2048]{0:T(1024)S(1)}, f32[2048]{0:T(1024)}, u32[]{:S(2)}) copy-start(f32[2048]{0:T(1024)} %param.6) | copy-start | bytes 24580
  33.4 109.2 %all-reduce.11.cloned.1.call-start = ((), (), s32[]{:S(2)}) async-start(), calls=%async_computation.1 | async-start | bytes 1179648 | tf_op jit(solution)/shard_map/psum | solution.py:56
  89.9 1.6 copy-start.3
  103.5 106.6 %all-reduce.13.cloned.1.call-start = ((), (), s32[]{:S(2)}) async-start(), calls=%async_computation.2 | async-start | bytes 2228224 | tf_op jit(solution)/shard_map/psum | solution.py:21
  153.5 110.2 %all-reduce.15.cloned.1.call-start = ((), (), s32[]{:S(2)}) async-start(), calls=%async_computation.3 | async-start | bytes 1179648 | tf_op jit(solution)/shard_map/psum | solution.py:56
  210.1 2.7 copy-start.1
  224.6 106.7 %all-reduce.17.cloned.1.call-start = ((), (), s32[]{:S(2)}) async-start(), calls=%async_computation.4 | async-start | bytes 2228224 | tf_op jit(solution)/shard_map/psum | solution.py:21
  274.7 110.2 %all-reduce.19.cloned.1.call-start = ((), (), s32[]{:S(2)}) async-start(), calls=%async_computation.5 | async-start | bytes 1179648 | tf_op jit(solution)/shard_map/psum | solution.py:56
  331.3 2.7 copy-start.2
  345.8 106.7 %all-reduce.21.cloned.1.call-start = ((), (), s32[]{:S(2)}) async-start(), calls=%async_computation.6 | async-start | bytes 2228224 | tf_op jit(solution)/shard_map/psum | solution.py:21
  395.8 110.2 %all-reduce.23.cloned.1.call-start = ((), (), s32[]{:S(2)}) async-start(), calls=%async_computation.7 | async-start | bytes 1179648 | tf_op jit(solution)/shard_map/psum | solution.py:56
  452.5 2.7 copy-start
Sparse Core Ops, SparseCore 0:
  33.5 56.3 all-reduce.8
  103.7 38.9 all-reduce.10
  153.6 56.4 all-reduce.12
  224.7 38.9 all-reduce.14
  274.8 56.4 all-reduce.16
  345.9 38.9 all-reduce.18
  396.0 56.4 all-reduce.20
  467.1 38.9 all-reduce.22
where the time goes:
time: 531 us
  waiting for transfers between devices  382 us (72%)
  matrix products  71.9 us (14%)
  blocking collectives  28.1 us (5%)
  other arithmetic  26.1 us (5%)
  between operations  14.3 us (3%)
  local copies, waits for them, and re-layouts  7.71 us (1%)
    psum x4, waiting for transfers between devices, project(): return lax.psum(projected, 'ka')  226 us
    psum x4, waiting for transfers between devices, per_device(): combined = lax.psum(combine_partial_value, 'ga')  156 us
    dot_general x4, matrix products, per_device(): jnp.dot(pair_densities, weighted, precision=precise, preferred_element_ty...  43.8 us
    dot_general x4, matrix products, project(): jnp.dot(pair_densities.T, full_vector, precision=precise, preferred_eleme...  28.1 us
    psum x1, blocking collectives, per_device(): start_sq = lax.psum(jnp.sum(start * start, axis=0), 'ka')  15.2 us
    psum x1, blocking collectives, per_device(): last_sq = lax.psum(jnp.sum(remainder_own * remainder_own, axis=0), 'ka')  13 us
  transfers between devices with their start and end apart: 8, of which 8 were waited for; matrix products, arithmetic and copies ran while one was open for 0% of the time, Pallas kernels for 0%

commit v1 on v0

v1 whole, which is shorter than its diff:
```python
import functools

import jax
import jax.numpy as jnp
from jax import lax
from jax.experimental import pallas as pl
from jax.experimental.pallas import tpu as pltpu
from jax.sharding import PartitionSpec as P

ITERS = 4
EPSILON = 1e-06
MESH = pl.DeviceIdType.MESH
F32 = jnp.float32
BF16 = jnp.bfloat16
NT = (((1,), (1,)), ((), ()))
NN = (((1,), (0,)), ((), ()))


def split(x):
    hi = x.astype(BF16)
    return hi, (x - hi.astype(F32)).astype(BF16)


def dot3(x_hi_lo, x_hi, w_hi, w_lo, dims):
    n = x_hi.shape[0]
    both = lax.dot_general(x_hi_lo, w_hi, dims, preferred_element_type=F32)
    low = lax.dot_general(x_hi, w_lo, dims, preferred_element_type=F32)
    return both[:n] + both[n:] + low


def kernel(nka, nga, cfg, m_ref, e_ref, c_ref, s_ref, al_ref, be_ref, out_ref,
           mhi, mlo, r, prev, xs, ws, tx, rx, acc, full, ypart, rtx, ltx, rrx, lrx,
           row_tx, ka_rx, ga_tx, ga_rx, *rest):
    nb, gw, cw, nch, nv = cfg
    stage_rx = rest[:nb]
    (core_ss, core_rs, st_ss, st_rs, ag_ss, ag_rs, fin_ss, fin_rs,
     r_ss, r_rs, l_ss, l_rs, ka_ss, ka_rs, ga_ss, ga_rs) = rest[nb:]
    ka = lax.axis_index("ka")
    ga = lax.axis_index("ga")
    core = ka % 2
    rows, gs = m_ref.shape
    gh = gs // 2

    def flip(mask):
        return ka + mask - 2 * mask * ((ka // mask) % 2)

    def bit_of(mask):
        return (ka // mask) % 2

    partners, bits = [], []
    for t in range(nb):
        a, b = 2 << t, 2 << (nb - 1 - t)
        partners.append(flip(a) + core * (flip(b) - flip(a)))
        bits.append(bit_of(a) + core * (bit_of(b) - bit_of(a)))

    barrier = pltpu.get_barrier_semaphore()
    for i in range(1, nka):
        pl.semaphore_signal(barrier, inc=1, device_id=((ka + i) % nka, ga), device_id_type=MESH)
    for i in range(1, nga):
        pl.semaphore_signal(barrier, inc=1, device_id=(ka, (ga + i) % nga), device_id_type=MESH)

    @pl.loop(0, rows // 128)
    def _(i):
        sl = pl.ds(pl.multiple_of(i * 128, 128), 128)
        hi, lo = split(m_ref[sl, :])
        mhi[sl, :] = hi
        mlo[sl, :] = lo
        r[:, sl] = s_ref[sl, :].T

    prev[...] = jnp.zeros_like(prev)
    pl.semaphore_wait(barrier, nka - 1 + nga - 1)

    def copy(src, dst, ss, rs, dev):
        return pltpu.make_async_remote_copy(
            src_ref=src, dst_ref=dst, send_sem=ss, recv_sem=rs, device_id=dev, device_id_type=MESH)

    def fold(x):
        parts = x[:, :128]
        for i in range(1, x.shape[1] // 128):
            parts = parts + x[:, i * 128:(i + 1) * 128]
        return jnp.sum(parts.T, axis=0, keepdims=True)

    def column(row):
        return jnp.broadcast_to(row, (128, nv)).T

    def wide(col, width):
        return jnp.concatenate([col] * (width // 128), axis=1)

    def small_copies(src, dst, ss, rs, n, me, dev, par):
        return [copy(src.at[par], dst.at[par, i], ss.at[i], rs.at[par, i], dev((me + i) % n))
                for i in range(1, n)]

    def ka_small(par):
        return small_copies(row_tx, ka_rx, ka_ss, ka_rs, nka, ka, lambda d: (d, ga), par)

    def ga_small(par):
        return small_copies(ga_tx, ga_rx, ga_ss, ga_rs, nga, ga, lambda d: (ka, d), par)

    def finish(copies, src, dst, n, par):
        for c in copies:
            c.wait()
        total = src[par]
        for i in range(1, n):
            total = total + dst[par, i]
        return total

    def project(half, write):
        @pl.loop(0, gh // gw)
        def _(i):
            dst = pl.ds(pl.multiple_of(i * gw, gw), gw)
            sl = pl.ds(pl.multiple_of(half * gh + i * gw, gw), gw)
            write(dst, dot3(xs[...], xs[:nv, :], mhi[:, sl], mlo[:, sl], NN))

    def body(k, carry):
        par = k % 2
        x = r[...]
        hi, lo = split(x)
        xs[:nv, :] = hi
        xs[nv:, :] = lo
        sq = x * x
        row_tx[par, 0:1, :] = fold(sq)
        row_tx[par, 1:2, :] = fold(e_ref[...] * sq)
        sums = ka_small(par)
        for c in sums:
            c.start()

        def to_tx(dst, y):
            tx[:, dst] = y

        def to_acc(dst, y):
            acc[:, dst] = y

        other = ka + 1 - 2 * core
        project(1 - core, to_tx)
        first = copy(tx, rx.at[par], core_ss.at[0], core_rs.at[par], (other, ga))
        first.start()
        project(core, to_acc)
        first.wait()
        acc[...] += rx[par]

        off, size = 0, nv
        spans = []
        for t in range(nb - 1):
            size //= 2
            keep = pl.multiple_of(off + bits[t] * size, 8)
            give = pl.multiple_of(off + (1 - bits[t]) * size, 8)
            c = copy(acc.at[pl.ds(give, size), :], stage_rx[t].at[par], st_ss.at[t], st_rs.at[par, t],
                     (partners[t], ga))
            c.start()
            c.wait()
            acc[pl.ds(keep, size), :] += stage_rx[t][par]
            off = keep
            spans.append((keep, size))
        t = nb - 1
        mine = pl.ds(off, size)
        c = copy(acc.at[mine, :], stage_rx[t].at[par], st_ss.at[t], st_rs.at[par, t], (partners[t], ga))
        c.start()
        c.wait()
        full[par, core, mine, :] = acc[mine, :] + stage_rx[t][par]
        for t in reversed(range(nb - 1)):
            keep, size = spans[t]
            part = full.at[par, core, pl.ds(keep, size), :]
            c = copy(part, part, ag_ss.at[t], ag_rs.at[par, t], (partners[t], ga))
            c.start()
            c.wait()
        part = full.at[par, core]
        c = copy(part, part, fin_ss.at[0], fin_rs.at[par], (other, ga))
        c.start()

        total = finish(sums, row_tx, ka_rx, nka, par)
        beta = jnp.sqrt(total[0:1] + EPSILON)
        energy = total[1:2] / (beta * beta)
        be_ref[pl.ds(jnp.maximum(k - 1, 0), 1), :] = beta
        beta_col = column(beta)
        c.wait()

        curve = jnp.zeros((nv, 128), F32)
        for h in range(2):
            for i in range(gh // 128):
                sl = slice(i * 128, (i + 1) * 128)
                gsl = slice(h * gh + i * 128, h * gh + (i + 1) * 128)
                p = full[par, h, :, sl] / beta_col
                w = c_ref[:, gsl] * p
                curve = curve + p * w
                hi, lo = split(w)
                ws[:nv, gsl] = hi
                ws[nv:, gsl] = lo
        ga_tx[par, 0:1, :] = fold(curve)
        curves = ga_small(par)
        for c in curves:
            c.start()

        def right(j):
            return copy(rtx.at[j], rrx.at[par, j], r_ss.at[j], r_rs.at[par, j], (ka, ga + 1))

        def left(j):
            return copy(ltx.at[j], lrx.at[par, j], l_ss.at[j], l_rs.at[par, j], (ka, ga - 1))

        @pl.loop(0, nch)
        def _(j):
            sl = pl.ds(pl.multiple_of(j * cw, cw), cw)
            y = dot3(ws[...], ws[:nv, :], mhi[sl, :], mlo[sl, :], NT)
            ypart[j] = y

            @pl.when(ga == 0)
            def _():
                rtx[j] = y
                right(j).start()

            @pl.when(ga == nga - 1)
            def _():
                ltx[j] = y
                left(j).start()

        beta_wide = wide(beta_col, rows)
        r[...] = r[...] / beta_wide
        for j in range(nch):
            @pl.when(ga > 0)
            def _():
                right(j).wait_recv()

                @pl.when(ga < nga - 1)
                def _():
                    rtx[j] = rrx[par, j] + ypart[j]
                    right(j).start()

            @pl.when(ga < nga - 1)
            def _():
                left(j).wait_recv()

                @pl.when(ga > 0)
                def _():
                    ltx[j] = lrx[par, j] + ypart[j]
                    left(j).start()

        alpha = energy + finish(curves, ga_tx, ga_rx, nga, par)[0:1]
        al_ref[pl.ds(k, 1), :] = alpha
        alpha_col = wide(column(alpha), cw)
        beta_col = wide(beta_col, cw)
        for j in range(nch):
            sl = slice(j * cw, (j + 1) * cw)

            @pl.when(ga > 0)
            def _():
                ypart[j] += rrx[par, j]

            @pl.when(ga < nga - 1)
            def _():
                ypart[j] += lrx[par, j]

            v = r[:, sl]
            new = (e_ref[:, sl] - alpha_col) * v + ypart[j] - beta_col * prev[:, sl]
            prev[:, sl] = v
            r[:, sl] = new
        for j in range(nch):
            @pl.when(ga < nga - 1)
            def _():
                right(j).wait_send()

            @pl.when(ga > 0)
            def _():
                left(j).wait_send()
        return carry

    lax.fori_loop(0, ITERS, body, 0)
    par = ITERS % 2
    x = r[...]
    row_tx[par, 0:1, :] = fold(x * x)
    sums = ka_small(par)
    for c in sums:
        c.start()
    total = finish(sums, row_tx, ka_rx, nka, par)
    beta = jnp.sqrt(total[0:1] + EPSILON)
    be_ref[ITERS - 1:ITERS, :] = beta
    for j in range(rows // 128):
        sl = slice(j * 128, (j + 1) * 128)
        out_ref[sl, :] = r[:, sl].T / beta


def solution(mesh):
    nka, nga = mesh.shape["ka"], mesh.shape["ga"]
    nb = (nka // 2).bit_length() - 1

    def step(m, e, c, s):
        rows, gs = m.shape
        nv = s.shape[1]
        gh = gs // 2
        gw = min(512, gh)
        cw = 256
        nch = rows // cw
        stage = []
        for t in range(nb):
            size = nv >> (t + 1) if t < nb - 1 else nv >> (nb - 1)
            stage.append(pltpu.VMEM((2, size, gh), F32))
        vm = pltpu.VMEM
        dma = pltpu.SemaphoreType.DMA
        return pl.pallas_call(
            functools.partial(kernel, nka, nga, (nb, gw, cw, nch, nv)),
            out_shape=(jax.ShapeDtypeStruct((ITERS, nv), F32), jax.ShapeDtypeStruct((ITERS, nv), F32),
                       jax.ShapeDtypeStruct((rows, nv), F32)),
            in_specs=[pl.BlockSpec(memory_space=pltpu.VMEM)] * 4,
            out_specs=(pl.BlockSpec(memory_space=pltpu.VMEM),) * 3,
            scratch_shapes=[
                vm((rows, gs), BF16), vm((rows, gs), BF16), vm((nv, rows), F32), vm((nv, rows), F32),
                vm((2 * nv, rows), BF16), vm((2 * nv, gs), BF16),
                vm((nv, gh), F32), vm((2, nv, gh), F32), vm((nv, gh), F32), vm((2, 2, nv, gh), F32),
                vm((nch, nv, cw), F32), vm((nch, nv, cw), F32), vm((nch, nv, cw), F32),
                vm((2, nch, nv, cw), F32), vm((2, nch, nv, cw), F32),
                vm((2, 8, nv), F32), vm((2, nka, 8, nv), F32), vm((2, 8, nv), F32), vm((2, nga, 8, nv), F32),
            ] + stage + [
                dma((1,)), dma((2,)), dma((nb,)), dma((2, nb)), dma((nb,)), dma((2, nb)), dma((1,)), dma((2,)),
                dma((nch,)), dma((2, nch)), dma((nch,)), dma((2, nch)),
                dma((nka,)), dma((2, nka)), dma((nga,)), dma((2, nga)),
            ],
            compiler_params=pltpu.CompilerParams(
                collective_id=0, has_side_effects=True, vmem_limit_bytes=60 * 1024 * 1024),
        )(m, e[None, :], c[None, :], s)

    placed = (P("ka", "ga"), P("ka"), P("ga"), P("ka", None))
    return jax.shard_map(
        step, mesh=mesh, in_specs=placed, out_specs=(P(), P(), P("ka", None)), check_vma=False)
```

time: 531 us -> 275 us (0.52)
  waiting for transfers between devices: 382 us -> 0 us
  Pallas kernels: 0 us -> 270 us
  matrix products: 71.9 us -> 0 us
  blocking collectives: 28.1 us -> 0 us
  other arithmetic: 26.1 us -> 0 us
  between operations: 14.3 us -> 0.64 us
    psum x8 -> x0, waiting for transfers between devices: 382 us -> none  [the longest x4 226 us: project(): return lax.psum(projected, 'ka')]
    pallas_call x0 -> x1, Pallas kernels: none -> 270 us  [step(): pl.pallas_call(functools.partial(kernel, nka, nga, (nb, gw, cw, nch, nv))...]
    dot_general x8 -> x0, matrix products: 71.9 us -> none  [the longest x4 43.8 us: per_device(): jnp.dot(pair_densities, weighted, precision=precise, preferred_element_ty...]
    psum x2 -> x0, blocking collectives: 28.1 us -> none  [the longest x1 15.2 us: per_device(): start_sq = lax.psum(jnp.sum(start * start, axis=0), 'ka')]
    reduce_sum x10 -> x0, other arithmetic: 13.1 us -> none  [the longest x4 6.08 us: per_device(): curvature = jnp.sum(projected * weighted, axis=0)[None, :]]
  transfers between devices with their start and end apart: 8 -> 0, of which waited for: 8 -> 0; matrix products, arithmetic and copies ran while one was open for 0% -> 0% of each run, Pallas kernels for 0% -> 0%
where the time goes in v1:
time: 275 us
  Pallas kernels  270 us (98%)
  local copies, waits for them, and re-layouts  4.37 us (2%)
    pallas_call x1, Pallas kernels, step(): pl.pallas_call(functools.partial(kernel, nka, nga, (nb, gw, cw, nch, nv))...  270 us

profile of v1, /device:TPU:0, one launch (start us, length us, event | category | flops | bytes accessed | tf_op | source)
XLA Modules:
  0.0 274.6 jit_solution(16153731753758786779)
XLA Ops:
  0.6 269.6 %shard_map.67 = (f32[4,128]{1,0:T(4,128)}, f32[4,128]{1,0:T(4,128)}, f32[1024,128]{1,0:T(8,128)}) custom-call(f32[1024,2048]{1,0:T(8,128)} %m_ref.1, f32[1,1024]{1,0:T(1,128)} %bitcast.3, f32[1,2048]{1,0:T(1,128)} %bitcast.2, f32[1024,128]{1,0:T(8,128)} %s_ref.1), custom_call_target="tpu_custom_call" | custom-call | tf_op jit(solution)/shard_map/pallas_call | solution.py:297
  270.3 1.3 copy.10
  271.5 1.2 copy.11
  272.8 1.9 copy.12

commit v2 on v1

--- a/solution.py
+++ b/solution.py
@@ -200,38 +200,45 @@
         def _(j):
             sl = pl.ds(pl.multiple_of(j * cw, cw), cw)
             y = dot3(ws[...], ws[:nv, :], mhi[sl, :], mlo[sl, :], NT)
-            ypart[j] = y
-
-            @pl.when(ga == 0)
-            def _():
-                rtx[j] = y
-                right(j).start()
-
-            @pl.when(ga == nga - 1)
-            def _():
-                ltx[j] = y
-                left(j).start()
+            for h in range(2):
+                i = 2 * j + h
+                part = y[h * nv // 2:(h + 1) * nv // 2]
+                ypart[i] = part
+
+                @pl.when(ga == 0)
+                def _():
+                    rtx[i] = part
+                    right(i).start()
+
+                @pl.when(ga == nga - 1)
+                def _():
+                    ltx[i] = part
+                    left(i).start()
 
         beta_wide = wide(beta_col, rows)
         r[...] = r[...] / beta_wide
-        for j in range(nch):
-            @pl.when(ga > 0)
+        @pl.loop(0, 2 * nch + nga - 1)
+        def _(t):
+            jr = t - ga
+            jl = t - (nga - 1 - ga)
+
+            @pl.when((ga > 0) & (jr >= 0) & (jr < 2 * nch))
             def _():
-                right(j).wait_recv()
+                right(jr).wait_recv()
 
                 @pl.when(ga < nga - 1)
                 def _():
-                    rtx[j] = rrx[par, j] + ypart[j]
-                    right(j).start()
-
-            @pl.when(ga < nga - 1)
+                    rtx[jr] = rrx[par, jr] + ypart[jr]
+                    right(jr).start()
+
+            @pl.when((ga < nga - 1) & (jl >= 0) & (jl < 2 * nch))
             def _():
-                left(j).wait_recv()
+                left(jl).wait_recv()
 
                 @pl.when(ga > 0)
                 def _():
-                    ltx[j] = lrx[par, j] + ypart[j]
-                    left(j).start()
+                    ltx[jl] = lrx[par, jl] + ypart[jl]
+                    left(jl).start()
 
         alpha = energy + finish(curves, ga_tx, ga_rx, nga, par)[0:1]
         al_ref[pl.ds(k, 1), :] = alpha
@@ -240,19 +247,21 @@
         for j in range(nch):
             sl = slice(j * cw, (j + 1) * cw)
 
-            @pl.when(ga > 0)
-            def _():
-                ypart[j] += rrx[par, j]
-
-            @pl.when(ga < nga - 1)
-            def _():
-                ypart[j] += lrx[par, j]
+            for i in (2 * j, 2 * j + 1):
+                @pl.when(ga > 0)
+                def _():
+                    ypart[i] += rrx[par, i]
+
+                @pl.when(ga < nga - 1)
+                def _():
+                    ypart[i] += lrx[par, i]
 
             v = r[:, sl]
-            new = (e_ref[:, sl] - alpha_col) * v + ypart[j] - beta_col * prev[:, sl]
+            mixed = jnp.concatenate([ypart[2 * j], ypart[2 * j + 1]], axis=0)
+            new = (e_ref[:, sl] - alpha_col) * v + mixed - beta_col * prev[:, sl]
             prev[:, sl] = v
             r[:, sl] = new
-        for j in range(nch):
+        for j in range(2 * nch):
             @pl.when(ga < nga - 1)
             def _():
                 right(j).wait_send()
@@ -304,12 +313,12 @@
                 vm((rows, gs), BF16), vm((rows, gs), BF16), vm((nv, rows), F32), vm((nv, rows), F32),
                 vm((2 * nv, rows), BF16), vm((2 * nv, gs), BF16),
                 vm((nv, gh), F32), vm((2, nv, gh), F32), vm((nv, gh), F32), vm((2, 2, nv, gh), F32),
-                vm((nch, nv, cw), F32), vm((nch, nv, cw), F32), vm((nch, nv, cw), F32),
-                vm((2, nch, nv, cw), F32), vm((2, nch, nv, cw), F32),
+                vm((2 * nch, nv // 2, cw), F32), vm((2 * nch, nv // 2, cw), F32), vm((2 * nch, nv // 2, cw), F32),
+                vm((2, 2 * nch, nv // 2, cw), F32), vm((2, 2 * nch, nv // 2, cw), F32),
                 vm((2, 8, nv), F32), vm((2, nka, 8, nv), F32), vm((2, 8, nv), F32), vm((2, nga, 8, nv), F32),
             ] + stage + [
                 dma((1,)), dma((2,)), dma((nb,)), dma((2, nb)), dma((nb,)), dma((2, nb)), dma((1,)), dma((2,)),
-                dma((nch,)), dma((2, nch)), dma((nch,)), dma((2, nch)),
+                dma((2 * nch,)), dma((2, 2 * nch)), dma((2 * nch,)), dma((2, 2 * nch)),
                 dma((nka,)), dma((2, nka)), dma((nga,)), dma((2, nga)),
             ],
             compiler_params=pltpu.CompilerParams(

time: 275 us -> 222 us (0.81)
  Pallas kernels: 270 us -> 216 us
    pallas_call x1, Pallas kernels: 270 us -> 216 us  [step(): pl.pallas_call(functools.partial(kernel, nka, nga, (nb, gw, cw, nch, nv))...]
where the time goes in v2:
time: 222 us; the launch traced here: 221 us
  Pallas kernels  216 us (97%)
  local copies, waits for them, and re-layouts  4.37 us (2%)
    pallas_call x1, Pallas kernels, step(): pl.pallas_call(functools.partial(kernel, nka, nga, (nb, gw, cw, nch, nv))...  216 us

profile of v2, /device:TPU:0, one launch (start us, length us, event | category | flops | bytes accessed | tf_op | source)
XLA Modules:
  0.0 221.4 jit_solution(8442119389684740729)
XLA Ops:
  0.6 216.4 %shard_map.67 = (f32[4,128]{1,0:T(4,128)}, f32[4,128]{1,0:T(4,128)}, f32[1024,128]{1,0:T(8,128)}) custom-call(f32[1024,2048]{1,0:T(8,128)} %m_ref.1, f32[1,1024]{1,0:T(1,128)} %bitcast.3, f32[1,2048]{1,0:T(1,128)} %bitcast.2, f32[1024,128]{1,0:T(8,128)} %s_ref.1), custom_call_target="tpu_custom_call" | custom-call | tf_op jit(solution)/shard_map/pallas_call | solution.py:306
  217.0 1.3 copy.10
  218.3 1.2 copy.11
  219.5 1.9 copy.12
